TPU v7x, 256 devices: a whole 4x4x8 slice. The times are simulated.
256 devices in a mesh: freq: 128 (over x, z, y_hi, core), row: 2 (over y_lo).
Axes of the slice: x: 4, y: 4 (y_hi: 2, y_lo: 2; y = y_hi * 2 + y_lo), z: 8, core: 2. Of those that a mesh axis runs over, the one named last changes fastest.
Arguments:
- reflect_re: float32 [128, 1728, 1728], P('freq', 'row'), may hold values from -0.046875 to 0.046875
- reflect_im: float32 [128, 1728, 1728], P('freq', 'row'), may hold values from -0.046875 to 0.046875
- focus_re: float32 [128, 1728, 32], P('freq', 'row'), may hold values from -6 to 6
- focus_im: float32 [128, 1728, 32], P('freq', 'row'), may hold values from -6 to 6
- first_arrival: int32 [1728, 32], P('row'), may hold values from 32 to 127
Outputs:
- minus_re: float32 [128, 1728, 32], P('freq', 'row')
- minus_im: float32 [128, 1728, 32], P('freq', 'row')
- plus_re: float32 [128, 1728, 32], P('freq', 'row')
- plus_im: float32 [128, 1728, 32], P('freq', 'row')
All inputs are finite; a program needn't handle non-finite values.
Results may differ from a plain program's by a relative error of at most 0.0001.
Values sent between devices are 32-bit elements; how exact they have to be, the bound alone decides.
A program may use at most 128 MiB of HBM per device.

v0:
```python
import functools
import math

import jax
import jax.numpy as jnp
import numpy as np
from jax import lax
from jax.experimental import pallas as pl
from jax.experimental.pallas import tpu as pltpu
from jax.sharding import PartitionSpec as P

MESH = pl.DeviceIdType.MESH
ITERS = 4
F32 = jnp.float32
BF16 = jnp.bfloat16
BLK = 216
CHUNK = 96


def split_np(table):
    hi = table.astype(jnp.bfloat16)
    lo = (table - hi.astype(np.float64)).astype(hi.dtype)
    return hi, lo


def tables():
    order = np.array(
        [
            x * 32 + z * 4 + y * 2 + c
            for z in range(8)
            for x in range(4)
            for y in range(2)
            for c in range(2)
        ]
    )
    t = np.arange(256)
    angle = 2.0 * math.pi * ((t[:, None] * order[None, :]) % 256) / 256
    weight = np.where(order == 0, 1.0 / 256, 2.0 / 256)
    t1 = np.concatenate([np.cos(angle) * weight, -np.sin(angle) * weight], axis=1)
    t2 = np.concatenate([np.cos(angle).T, -np.sin(angle).T], axis=0)
    out = []
    for table in (t1, t2):
        hi, lo = split_np(table)
        out.append(np.concatenate([hi, lo, hi], axis=1))
    return out


def split(v):
    hi = v.astype(BF16)
    lo = (v - hi.astype(F32)).astype(BF16)
    return hi, lo


def copies(src, dst, ssem, rsem, dev):
    return pltpu.make_async_remote_copy(
        src_ref=src, dst_ref=dst, send_sem=ssem, recv_sem=rsem, device_id=dev, device_id_type=MESH
    )


def wait_bytes(ref, sem):
    pltpu.make_async_copy(ref, ref, sem).wait()


def kernel(
    rre, rim, fre, fim, fa, t1, t2,
    mre, mim, pre, pim,
    stage, rcat, acc, fsend, relay1, gbuf, bsend, relay2, urecv, fasend, farecv,
    ld_sem, ini_send, ini_recv, fa_send, fa_recv,
    f1_send, f1_recv, f2_send, f2_recv, b1_send, b1_recv, b2_send, b2_send2, b2_recv,
):
    me = lax.axis_index("freq")
    row = lax.axis_index("row")
    x = me // 32
    z = (me // 4) % 8
    yh = (me // 2) % 2
    c = me % 2
    ypos = 2 * yh + row
    xs = [lax.rem(x + d, 4) for d in range(4)]
    zs = [lax.rem(z + d, 8) for d in range(8)]
    ys = [lax.rem(ypos + d, 4) for d in range(4)]
    cs = [c, 1 - c]

    def dev(xi, zi, yi, ci):
        return (xi * 32 + zi * 4 + (yi // 2) * 2 + ci, lax.rem(yi, 2))

    plane = [(dx, dy, dc) for dx in (2, 1, 3, 0) for dy in (2, 1, 3, 0) for dc in (1, 0)][:-1]
    zorder = [4, 3, 5, 2, 6, 1, 7]
    barrier = pltpu.get_barrier_semaphore()
    for dx, dy, dc in plane:
        pl.semaphore_signal(
            barrier, inc=1, device_id=dev(xs[dx], z, ys[dy], cs[dc]), device_id_type=MESH
        )
    for dz in zorder:
        pl.semaphore_signal(barrier, inc=1, device_id=dev(x, zs[dz], ypos, c), device_id_type=MESH)

    nchunk = rre.shape[0] // CHUNK
    for k in range(nchunk):
        for a, ref in enumerate((rre, rim)):
            pltpu.make_async_copy(
                ref.at[pl.ds(k * CHUNK, CHUNK)],
                stage.at[a, pl.ds(k * CHUNK, CHUNK)],
                ld_sem.at[k, a],
            ).start()

    u2 = urecv.reshape(5 * 8 * 128, 128)
    for q in range(4):
        base = (row * 4 + q) * 128
        for h in range(2):
            n = 128 if h == 0 else BLK - 128
            rows = pl.ds(BLK * q + 128 * h, n)
            both = jnp.concatenate([fre[rows, :], fim[rows, :], jnp.zeros((n, 64), F32)], axis=1)
            if n < 128:
                both = jnp.concatenate([both, jnp.zeros((128 - n, 128), F32)], axis=0)
            both = both.T
            for ri in range(2):
                u2[pl.ds(base + 2 * h + ri, 32, stride=4), :] = both[32 * ri : 32 * ri + 32]
    myq = 2 * yh + c
    myp = x * 8 + z
    pick = lax.broadcasted_iota(jnp.int32, (128, 128), 0) == myp
    for h in range(2):
        n = 128 if h == 0 else BLK - 128
        rows = pl.ds(pl.multiple_of(BLK * myq + 128 * h, 8), n)
        v = jnp.concatenate([fa[rows, :].astype(F32), jnp.zeros((n, 96), F32)], axis=1)
        if n < 128:
            v = jnp.concatenate([v, jnp.zeros((128 - n, 128), F32)], axis=0)
        v = jnp.sum(jnp.where(pick, v.T, 0.0), axis=0, keepdims=True)
        fasend[8 * h : 8 * h + 8] = jnp.broadcast_to(v, (8, 128))

    pl.semaphore_wait(barrier, len(plane) + len(zorder))
    partner = (me, 1 - row)
    mine = urecv.at[0, pl.ds(row * 4, 4)]
    ini = copies(mine, mine, ini_send, ini_recv, partner)
    ini.start()
    fac = copies(fasend, farecv, fa_send, fa_recv, partner)
    fac.start()

    def convert(k, carry):
        rows = pl.ds(pl.multiple_of(k * CHUNK, CHUNK), CHUNK)
        for a in range(2):
            wait_bytes(stage.at[a, pl.ds(0, CHUNK)], ld_sem.at[k, a])
            for b in range(8):
                v = stage[a, rows, BLK * b : BLK * b + BLK]
                v = jnp.concatenate([v, jnp.zeros((CHUNK, 256 - BLK), F32)], axis=1)
                hi, lo = split(v)
                rcat[b, rows, 512 * a : 512 * a + 256] = hi
                rcat[b, rows, 512 * a + 256 : 512 * a + 512] = lo
        return carry

    lax.fori_loop(0, nchunk, convert, 0)
    acc[864:, :] = jnp.zeros_like(acc[864:, :])
    ini.wait()
    fac.wait()

    f1v = fsend.reshape(ITERS * 512, 128)
    g2 = gbuf.reshape(ITERS * 512, 128)
    bs2 = bsend.reshape(ITERS * 512, 128)
    ublk = urecv.reshape(5 * 32, 8, 4, 128)
    sid = (x * 2 + yh) * 2 + c
    myn = (1 - row) * 4 + myq
    reach = jnp.concatenate([farecv[0:1], farecv[8:9]], axis=1)
    tid = lax.broadcasted_iota(jnp.int32, (256, 256), 0)
    dist = jnp.minimum(tid, 256 - tid).astype(F32)

    def apply(it, carry):
        sign = 1.0 - 2.0 * lax.rem(it, 2).astype(F32)
        extra = jnp.where(it == 2, 1.0, 0.0).astype(F32)

        def block(dy, dc, first):
            yi = lax.rem(ypos + dy, 4)
            ci = lax.rem(c + dc, 2)
            n = (1 - lax.rem(yi, 2)) * 4 + (yi // 2) * 2 + ci

            @pl.when(it > 0)
            def _():
                if first:
                    wait_bytes(urecv.at[it, n, pl.ds(0, 3)], b2_recv.at[it, n])
                else:
                    wait_bytes(urecv.at[it, n], b2_recv.at[it, n])

            parts = []
            for ri in range(2):
                halves = []
                for h in range(2):
                    j = 2 * h + ri
                    now = u2[pl.ds((it * 8 + n) * 128 + j, 32, stride=4), :]
                    start = u2[pl.ds(n * 128 + j, 32, stride=4), :]
                    halves.append(now + extra * start)
                parts.append(jnp.concatenate(halves, axis=1))
            ur, ui = parts
            urh, url = split(ur)
            uih, uil = split(ui)
            sg = sign.astype(BF16)
            w1 = jnp.concatenate([urh, uih, url, uil], axis=0)
            w2 = jnp.concatenate([-(sg * uih), sg * urh, -(sg * uil), sg * url], axis=0)
            w = jnp.concatenate([w1, w1, w2, w2], axis=1)
            part = lax.dot_general(
                rcat[n], w, (((1,), (1,)), ((), ())), preferred_element_type=F32
            )
            if first:
                acc[0:864, :] = part
            else:
                acc[0:864, :] += part

        block(0, 0, True)

        def rest(t, carry):
            v = t // 2
            dy = v + v // 2 - 2 * (v // 3)
            block(dy, lax.rem(t, 2), False)
            return carry

        lax.fori_loop(1, 8, rest, 0)

        for q in range(4):
            for h in range(2):
                v = acc[BLK * q + 128 * h : BLK * q + 128 * h + 128, :].T
                v = v[0:64] + v[64:128]
                for ri in range(2):
                    f1v[pl.ds(it * 512 + q * 128 + 2 * h + ri, 32, stride=4), :] = v[
                        32 * ri : 32 * ri + 32
                    ]
            for dx in (2, 1, 3, 0):
                copies(
                    fsend.at[it, q, xs[dx]],
                    relay1.at[it, sid],
                    f1_send.at[it],
                    f1_recv.at[it],
                    dev(xs[dx], z, 2 * (q // 2) + 1 - row, q % 2),
                ).start()
        wait_bytes(relay1.at[it], f1_recv.at[it])
        for dz in zorder:
            copies(
                relay1.at[it, :, zs[dz]],
                gbuf.at[it, z],
                f2_send.at[it],
                f2_recv.at[it],
                dev(x, zs[dz], ypos, c),
            ).start()
        gbuf[it, z] = relay1[it, :, z]
        wait_bytes(gbuf.at[it, pl.ds(0, 7)], f2_recv.at[it])

        g = jnp.concatenate(
            [
                jnp.concatenate(
                    [g2[pl.ds(it * 512 + 2 * h + ri, 128, stride=4), :] for h in range(2)], axis=1
                )
                for ri in range(2)
            ],
            axis=0,
        )
        gh, gl = split(g)
        tr = jnp.dot(t1[...], jnp.concatenate([gh, gh, gl], axis=0), preferred_element_type=F32)
        tr = jnp.where(dist < reach, tr, 0.0)
        th, tl = split(tr)
        out = jnp.dot(t2[...], jnp.concatenate([th, th, tl], axis=0), preferred_element_type=F32)
        for h in range(2):
            for ri in range(2):
                bs2[pl.ds(it * 512 + 2 * h + ri, 128, stride=4), :] = out[
                    128 * ri : 128 * ri + 128, 128 * h : 128 * h + 128
                ]
        for dz in zorder:
            copies(
                bsend.at[it, zs[dz]],
                relay2.at[it, z],
                b1_send.at[it],
                b1_recv.at[it],
                dev(x, zs[dz], ypos, c),
            ).start()
        relay2[it, z] = bsend[it, z]
        wait_bytes(relay2.at[it, pl.ds(0, 7)], b1_recv.at[it])

        def out_to(dx, dy, dc, sem):
            yi = ys[dy]
            s = (xs[dx] * 2 + yi // 2) * 2 + cs[dc]
            copies(
                relay2.at[it, :, s],
                urecv.at[it + 1, myn, x],
                sem,
                b2_recv.at[it + 1, myn],
                dev(xs[dx], z, yi, cs[dc]),
            ).start()

        for dx, dy, dc in plane:
            if dy % 2 == 1:
                out_to(dx, dy, dc, b2_send.at[it])

        @pl.when(it < ITERS - 1)
        def _():
            for dx, dy, dc in plane:
                if dy % 2 == 0:
                    out_to(dx, dy, dc, b2_send2.at[it])
            urecv[it + 1, myn, x] = relay2[it, :, sid]

        wait_bytes(fsend.at[it], f1_send.at[it])
        wait_bytes(gbuf.at[it, pl.ds(0, 7)], f2_send.at[it])
        wait_bytes(relay2.at[it, pl.ds(0, 7)], b1_send.at[it])
        wait_bytes(ublk.at[pl.ds(0, 16)], b2_send.at[it])

        @pl.when(it < ITERS - 1)
        def _():
            wait_bytes(ublk.at[pl.ds(0, 15)], b2_send2.at[it])

        return carry

    lax.fori_loop(0, ITERS, apply, 0)

    for q in range(4):
        n = row * 4 + q
        wait_bytes(urecv.at[ITERS, n], b2_recv.at[ITERS, n])
        for slot, outs in ((ITERS - 1, (mre, mim)), (ITERS, (pre, pim))):
            for h in range(2):
                m = 128 if h == 0 else BLK - 128
                vals = []
                for ri in range(2):
                    j = 2 * h + ri
                    v = u2[pl.ds((slot * 8 + n) * 128 + j, 32, stride=4), :]
                    if slot == ITERS:
                        v = v + u2[pl.ds(n * 128 + j, 32, stride=4), :]
                    vals.append(v)
                vals.append(jnp.zeros((64, 128), F32))
                v = jnp.concatenate(vals, axis=0).T
                rows = pl.ds(BLK * q + 128 * h, m)
                outs[0][rows, :] = v[0:m, 0:32]
                outs[1][rows, :] = v[0:m, 32:64]


def local(reflect_re, reflect_im, focus_re, focus_im, first_arrival):
    rows, cols = reflect_re.shape[1:]
    t1, t2 = tables()
    vmem = pl.BlockSpec(memory_space=pltpu.VMEM)
    hbm = pl.BlockSpec(memory_space=pl.ANY)
    dma = pltpu.SemaphoreType.DMA
    outs = pl.pallas_call(
        kernel,
        out_shape=[jax.ShapeDtypeStruct((rows, 32), F32)] * 4,
        in_specs=[hbm, hbm] + [vmem] * 5,
        out_specs=[vmem] * 4,
        scratch_shapes=[
            pltpu.VMEM((2, rows, cols), F32),
            pltpu.VMEM((8, rows, 1024), BF16),
            pltpu.VMEM((rows + 48, 128), F32),
            pltpu.VMEM((ITERS, 4, 4, 8, 4, 128), F32),
            pltpu.VMEM((ITERS, 16, 8, 4, 128), F32),
            pltpu.VMEM((ITERS, 8, 16, 4, 128), F32),
            pltpu.VMEM((ITERS, 8, 16, 4, 128), F32),
            pltpu.VMEM((ITERS, 8, 16, 4, 128), F32),
            pltpu.VMEM((5, 8, 4, 8, 4, 128), F32),
            pltpu.VMEM((16, 128), F32),
            pltpu.VMEM((16, 128), F32),
            dma((rows // CHUNK, 2)),
            dma, dma, dma, dma,
            dma((ITERS,)), dma((ITERS,)), dma((ITERS,)), dma((ITERS,)),
            dma((ITERS,)), dma((ITERS,)), dma((ITERS,)), dma((ITERS,)),
            dma((5, 8)),
        ],
        compiler_params=pltpu.CompilerParams(
            collective_id=0, has_side_effects=True, vmem_limit_bytes=60 * 1024 * 1024
        ),
    )(
        reflect_re[0], reflect_im[0], focus_re[0], focus_im[0], first_arrival,
        jnp.asarray(t1), jnp.asarray(t2),
    )
    return tuple(o[None] for o in outs)


def solution(mesh):
    placed = (
        P("freq", "row", None),
        P("freq", "row", None),
        P("freq", "row", None),
        P("freq", "row", None),
        P("row", None),
    )
    return jax.shard_map(
        local,
        mesh=mesh,
        in_specs=placed,
        out_specs=(P("freq", "row", None),) * 4,
        check_vma=False,
    )
```

profile of v0, /device:TPU:1, one launch (start us, length us, event | category | flops | bytes accessed | tf_op | source)
XLA Modules:
  0.0 172.3 jit_solution(1718709113524002068)
XLA Ops:
  0.6 1.9 %copy.11 = f32[1,864,32]{2,1,0:T(8,128)} copy(f32[1,864,32]{1,2,0:T(8,128)} %param.9) | data formatting | bytes 221184 | tf_op args[2]
  2.5 1.9 %copy.12 = f32[1,864,32]{2,1,0:T(8,128)} copy(f32[1,864,32]{1,2,0:T(8,128)} %param.10) | data formatting | bytes 221184 | tf_op args[3]
  4.4 1.9 %copy.13.fa = s32[864,32]{1,0:T(8,128)} copy(s32[864,32]{0,1:T(8,128)} %param.11) | data formatting | bytes 221184 | tf_op args[4]
  6.2 158.7 %shard_map.102 = (f32[864,32]{1,0:T(8,128)}, f32[864,32]{1,0:T(8,128)}, f32[864,32]{1,0:T(8,128)}, f32[864,32]{1,0:T(8,128)}) custom-call(f32[864,1728]{1,0:T(8,128)} %bitcast.8, f32[864,1728]{1,0:T(8,128)} %bitcast.9, f32[864,32]{1,0:T(8,128)} %bitcast.10, f32[864,32]{1,0:T(8,128)} %bitcast.11, s32[864,32]{1,0:T(8,128)} %copy.13.fa, ...), custom_call_target="tpu_custom_call" | custom-call | tf_op jit(solution)/shard_map/pallas_call | solution.py:333
  164.9 1.8 %copy.14 = f32[1,864,32]{1,2,0:T(8,128)} copy(f32[1,864,32]{2,1,0:T(8,128)} %bitcast.15) | data formatting | bytes 221184
  166.8 1.8 %copy.15 = f32[1,864,32]{1,2,0:T(8,128)} copy(f32[1,864,32]{2,1,0:T(8,128)} %bitcast.14) | data formatting | bytes 221184
  168.6 1.8 %copy.16 = f32[1,864,32]{1,2,0:T(8,128)} copy(f32[1,864,32]{2,1,0:T(8,128)} %bitcast.13) | data formatting | bytes 221184
  170.4 1.8 %copy.17 = f32[1,864,32]{1,2,0:T(8,128)} copy(f32[1,864,32]{2,1,0:T(8,128)} %bitcast.12) | data formatting | bytes 221184
where the time goes:
time: 173 us; the launch traced here: 172 us
  Pallas kernels  159 us (92%)
  local copies, waits for them, and re-layouts  13 us (8%)
    pallas_call x1, Pallas kernels, local(): pl.pallas_call(kernel, out_shape=[jax.ShapeDtypeStruct((rows, 32), F32)]...  159 us
    unnamed x7, local copies, waits for them, and re-layouts  13 us

commit v1 on v0

--- a/solution.py
+++ b/solution.py
@@ -28,8 +28,8 @@
         [
             x * 32 + z * 4 + y * 2 + c
             for z in range(8)
+            for y in range(2)
             for x in range(4)
-            for y in range(2)
             for c in range(2)
         ]
     )
@@ -107,24 +107,22 @@
         base = (row * 4 + q) * 128
         for h in range(2):
             n = 128 if h == 0 else BLK - 128
-            rows = pl.ds(BLK * q + 128 * h, n)
-            both = jnp.concatenate([fre[rows, :], fim[rows, :], jnp.zeros((n, 64), F32)], axis=1)
-            if n < 128:
-                both = jnp.concatenate([both, jnp.zeros((128 - n, 128), F32)], axis=0)
-            both = both.T
-            for ri in range(2):
-                u2[pl.ds(base + 2 * h + ri, 32, stride=4), :] = both[32 * ri : 32 * ri + 32]
+            lo = BLK * q + 128 * h
+            for ri, ref in enumerate((fre, fim)):
+                v = ref[:, lo : lo + n]
+                if n < 128:
+                    v = jnp.concatenate([v, jnp.zeros((32, 128 - n), F32)], axis=1)
+                u2[pl.ds(base + 2 * h + ri, 32, stride=4), :] = v
     myq = 2 * yh + c
     myp = x * 8 + z
-    pick = lax.broadcasted_iota(jnp.int32, (128, 128), 0) == myp
+    pick = lax.broadcasted_iota(jnp.int32, fa.shape, 0) == myp
+    v = jnp.sum(jnp.where(pick, fa[...].astype(F32), 0.0), axis=0, keepdims=True)
+    w = jnp.zeros((1, BLK), F32)
+    for q in range(4):
+        w = w + jnp.where(myq == q, v[:, BLK * q : BLK * q + BLK], 0.0)
+    w = jnp.concatenate([w, jnp.zeros((1, 256 - BLK), F32)], axis=1)
     for h in range(2):
-        n = 128 if h == 0 else BLK - 128
-        rows = pl.ds(pl.multiple_of(BLK * myq + 128 * h, 8), n)
-        v = jnp.concatenate([fa[rows, :].astype(F32), jnp.zeros((n, 96), F32)], axis=1)
-        if n < 128:
-            v = jnp.concatenate([v, jnp.zeros((128 - n, 128), F32)], axis=0)
-        v = jnp.sum(jnp.where(pick, v.T, 0.0), axis=0, keepdims=True)
-        fasend[8 * h : 8 * h + 8] = jnp.broadcast_to(v, (8, 128))
+        fasend[8 * h : 8 * h + 8] = jnp.broadcast_to(w[:, 128 * h : 128 * h + 128], (8, 128))
 
     pl.semaphore_wait(barrier, len(plane) + len(zorder))
     partner = (me, 1 - row)
@@ -148,14 +146,13 @@
 
     lax.fori_loop(0, nchunk, convert, 0)
     acc[864:, :] = jnp.zeros_like(acc[864:, :])
-    ini.wait()
     fac.wait()
 
     f1v = fsend.reshape(ITERS * 512, 128)
     g2 = gbuf.reshape(ITERS * 512, 128)
     bs2 = bsend.reshape(ITERS * 512, 128)
     ublk = urecv.reshape(5 * 32, 8, 4, 128)
-    sid = (x * 2 + yh) * 2 + c
+    sid = x * 2 + c
     myn = (1 - row) * 4 + myq
     reach = jnp.concatenate([farecv[0:1], farecv[8:9]], axis=1)
     tid = lax.broadcasted_iota(jnp.int32, (256, 256), 0)
@@ -165,17 +162,25 @@
         sign = 1.0 - 2.0 * lax.rem(it, 2).astype(F32)
         extra = jnp.where(it == 2, 1.0, 0.0).astype(F32)
 
-        def block(dy, dc, first):
-            yi = lax.rem(ypos + dy, 4)
-            ci = lax.rem(c + dc, 2)
+        def block(t, first):
+            v = t // 2
+            ci = lax.rem(c + t + 1, 2)
+            y_own = 2 * (v % 2) + lax.rem(row + 1 + v // 2, 2)
+            y_arr = 2 * lax.rem(yh + 1 + v // 2, 2) + lax.rem(row + 1 + v % 2, 2)
+            yi = jnp.where(it == 0, y_own, y_arr)
             n = (1 - lax.rem(yi, 2)) * 4 + (yi // 2) * 2 + ci
 
-            @pl.when(it > 0)
+            @pl.when((it > 0) & (t < 7))
             def _():
-                if first:
-                    wait_bytes(urecv.at[it, n, pl.ds(0, 3)], b2_recv.at[it, n])
-                else:
-                    wait_bytes(urecv.at[it, n], b2_recv.at[it, n])
+                wait_bytes(urecv.at[it, n], b2_recv.at[it, n])
+
+            @pl.when((it > 0) & (t == 7))
+            def _():
+                wait_bytes(urecv.at[it, n, pl.ds(0, 3)], b2_recv.at[it, n])
+
+            @pl.when((it == 0) & (t == 4))
+            def _():
+                ini.wait()
 
             parts = []
             for ri in range(2):
@@ -201,42 +206,45 @@
             else:
                 acc[0:864, :] += part
 
-        block(0, 0, True)
+        block(jnp.int32(0), True)
 
         def rest(t, carry):
-            v = t // 2
-            dy = v + v // 2 - 2 * (v // 3)
-            block(dy, lax.rem(t, 2), False)
+            block(t, False)
             return carry
 
         lax.fori_loop(1, 8, rest, 0)
 
-        for q in range(4):
-            for h in range(2):
-                v = acc[BLK * q + 128 * h : BLK * q + 128 * h + 128, :].T
-                v = v[0:64] + v[64:128]
-                for ri in range(2):
-                    f1v[pl.ds(it * 512 + q * 128 + 2 * h + ri, 32, stride=4), :] = v[
-                        32 * ri : 32 * ri + 32
-                    ]
-            for dx in (2, 1, 3, 0):
+        for dy in (1, 3):
+            yi = ys[dy]
+            for cd in range(2):
+                q = (yi // 2) * 2 + cd
+                for h in range(2):
+                    v = acc[pl.ds(pl.multiple_of(BLK * q + 128 * h, 8), 128), :].T
+                    v = v[0:64] + v[64:128]
+                    for ri in range(2):
+                        f1v[pl.ds(it * 512 + q * 128 + 2 * h + ri, 32, stride=4), :] = v[
+                            32 * ri : 32 * ri + 32
+                        ]
+                for dx in (2, 1, 3, 0):
+                    copies(
+                        fsend.at[it, q, xs[dx]],
+                        relay1.at[it, yh, sid],
+                        f1_send.at[it],
+                        f1_recv.at[it, yh],
+                        dev(xs[dx], z, yi, cd),
+                    ).start()
+        for dy in (3, 1):
+            v = ys[dy] // 2
+            wait_bytes(relay1.at[it, v], f1_recv.at[it, v])
+            for dz in zorder:
                 copies(
-                    fsend.at[it, q, xs[dx]],
-                    relay1.at[it, sid],
-                    f1_send.at[it],
-                    f1_recv.at[it],
-                    dev(xs[dx], z, 2 * (q // 2) + 1 - row, q % 2),
+                    relay1.at[it, v, :, zs[dz]],
+                    gbuf.at[it, z, v],
+                    f2_send.at[it],
+                    f2_recv.at[it],
+                    dev(x, zs[dz], ypos, c),
                 ).start()
-        wait_bytes(relay1.at[it], f1_recv.at[it])
-        for dz in zorder:
-            copies(
-                relay1.at[it, :, zs[dz]],
-                gbuf.at[it, z],
-                f2_send.at[it],
-                f2_recv.at[it],
-                dev(x, zs[dz], ypos, c),
-            ).start()
-        gbuf[it, z] = relay1[it, :, z]
+            gbuf[it, z, v] = relay1[it, v, :, z]
         wait_bytes(gbuf.at[it, pl.ds(0, 7)], f2_recv.at[it])
 
         g = jnp.concatenate(
@@ -258,42 +266,44 @@
                 bs2[pl.ds(it * 512 + 2 * h + ri, 128, stride=4), :] = out[
                     128 * ri : 128 * ri + 128, 128 * h : 128 * h + 128
                 ]
-        for dz in zorder:
+        for v in (1 - yh, yh):
+            for dz in zorder:
+                copies(
+                    bsend.at[it, zs[dz], v],
+                    relay2.at[it, v, z],
+                    b1_send.at[it],
+                    b1_recv.at[it, v],
+                    dev(x, zs[dz], ypos, c),
+                ).start()
+            relay2[it, v, z] = bsend[it, z, v]
+
+        def out_to(dx, v, r, dc, sem):
             copies(
-                bsend.at[it, zs[dz]],
-                relay2.at[it, z],
-                b1_send.at[it],
-                b1_recv.at[it],
-                dev(x, zs[dz], ypos, c),
-            ).start()
-        relay2[it, z] = bsend[it, z]
-        wait_bytes(relay2.at[it, pl.ds(0, 7)], b1_recv.at[it])
-
-        def out_to(dx, dy, dc, sem):
-            yi = ys[dy]
-            s = (xs[dx] * 2 + yi // 2) * 2 + cs[dc]
-            copies(
-                relay2.at[it, :, s],
+                relay2.at[it, v, :, xs[dx] * 2 + cs[dc]],
                 urecv.at[it + 1, myn, x],
                 sem,
                 b2_recv.at[it + 1, myn],
-                dev(xs[dx], z, yi, cs[dc]),
+                dev(xs[dx], z, 2 * v + r, cs[dc]),
             ).start()
 
-        for dx, dy, dc in plane:
-            if dy % 2 == 1:
-                out_to(dx, dy, dc, b2_send.at[it])
-
-        @pl.when(it < ITERS - 1)
-        def _():
-            for dx, dy, dc in plane:
-                if dy % 2 == 0:
-                    out_to(dx, dy, dc, b2_send2.at[it])
-            urecv[it + 1, myn, x] = relay2[it, :, sid]
+        for near, v in enumerate((1 - yh, yh)):
+            wait_bytes(relay2.at[it, v, pl.ds(0, 7)], b1_recv.at[it, v])
+            for dx in (2, 1, 3, 0):
+                for dc in (1, 0):
+                    out_to(dx, v, 1 - row, dc, b2_send.at[it])
+
+            @pl.when(it < ITERS - 1)
+            def _():
+                for dx in (2, 1, 3, 0):
+                    for dc in (1, 0):
+                        if near and dx == 0 and dc == 0:
+                            urecv[it + 1, myn, x] = relay2[it, v, :, sid]
+                        else:
+                            out_to(dx, v, row, dc, b2_send2.at[it])
 
         wait_bytes(fsend.at[it], f1_send.at[it])
         wait_bytes(gbuf.at[it, pl.ds(0, 7)], f2_send.at[it])
-        wait_bytes(relay2.at[it, pl.ds(0, 7)], b1_send.at[it])
+        wait_bytes(gbuf.at[it, pl.ds(0, 7)], b1_send.at[it])
         wait_bytes(ublk.at[pl.ds(0, 16)], b2_send.at[it])
 
         @pl.when(it < ITERS - 1)
@@ -310,18 +320,13 @@
         for slot, outs in ((ITERS - 1, (mre, mim)), (ITERS, (pre, pim))):
             for h in range(2):
                 m = 128 if h == 0 else BLK - 128
-                vals = []
+                lo = BLK * q + 128 * h
                 for ri in range(2):
                     j = 2 * h + ri
                     v = u2[pl.ds((slot * 8 + n) * 128 + j, 32, stride=4), :]
                     if slot == ITERS:
                         v = v + u2[pl.ds(n * 128 + j, 32, stride=4), :]
-                    vals.append(v)
-                vals.append(jnp.zeros((64, 128), F32))
-                v = jnp.concatenate(vals, axis=0).T
-                rows = pl.ds(BLK * q + 128 * h, m)
-                outs[0][rows, :] = v[0:m, 0:32]
-                outs[1][rows, :] = v[0:m, 32:64]
+                    outs[ri][:, lo : lo + m] = v[:, 0:m]
 
 
 def local(reflect_re, reflect_im, focus_re, focus_im, first_arrival):
@@ -332,7 +337,7 @@
     dma = pltpu.SemaphoreType.DMA
     outs = pl.pallas_call(
         kernel,
-        out_shape=[jax.ShapeDtypeStruct((rows, 32), F32)] * 4,
+        out_shape=[jax.ShapeDtypeStruct((32, rows), F32)] * 4,
         in_specs=[hbm, hbm] + [vmem] * 5,
         out_specs=[vmem] * 4,
         scratch_shapes=[
@@ -340,27 +345,27 @@
             pltpu.VMEM((8, rows, 1024), BF16),
             pltpu.VMEM((rows + 48, 128), F32),
             pltpu.VMEM((ITERS, 4, 4, 8, 4, 128), F32),
-            pltpu.VMEM((ITERS, 16, 8, 4, 128), F32),
-            pltpu.VMEM((ITERS, 8, 16, 4, 128), F32),
-            pltpu.VMEM((ITERS, 8, 16, 4, 128), F32),
-            pltpu.VMEM((ITERS, 8, 16, 4, 128), F32),
+            pltpu.VMEM((ITERS, 2, 8, 8, 4, 128), F32),
+            pltpu.VMEM((ITERS, 8, 2, 8, 4, 128), F32),
+            pltpu.VMEM((ITERS, 8, 2, 8, 4, 128), F32),
+            pltpu.VMEM((ITERS, 2, 8, 8, 4, 128), F32),
             pltpu.VMEM((5, 8, 4, 8, 4, 128), F32),
             pltpu.VMEM((16, 128), F32),
             pltpu.VMEM((16, 128), F32),
             dma((rows // CHUNK, 2)),
             dma, dma, dma, dma,
-            dma((ITERS,)), dma((ITERS,)), dma((ITERS,)), dma((ITERS,)),
-            dma((ITERS,)), dma((ITERS,)), dma((ITERS,)), dma((ITERS,)),
+            dma((ITERS,)), dma((ITERS, 2)), dma((ITERS,)), dma((ITERS,)),
+            dma((ITERS,)), dma((ITERS, 2)), dma((ITERS,)), dma((ITERS,)),
             dma((5, 8)),
         ],
         compiler_params=pltpu.CompilerParams(
             collective_id=0, has_side_effects=True, vmem_limit_bytes=60 * 1024 * 1024
         ),
     )(
-        reflect_re[0], reflect_im[0], focus_re[0], focus_im[0], first_arrival,
+        reflect_re[0], reflect_im[0], focus_re[0].T, focus_im[0].T, first_arrival.T,
         jnp.asarray(t1), jnp.asarray(t2),
     )
-    return tuple(o[None] for o in outs)
+    return tuple(o.T[None] for o in outs)
 
 
 def solution(mesh):

time: 173 us -> 153 us (0.88)
  Pallas kernels: 159 us -> 146 us
  local copies, waits for them, and re-layouts: 13 us -> 6.2 us
    pallas_call x1, Pallas kernels: 159 us -> 146 us  [local(): pl.pallas_call(kernel, out_shape=[jax.ShapeDtypeStruct((32, rows), F32)]...]
    unnamed x7 -> x4, local copies, waits for them, and re-layouts: 13 us -> 6.2 us
where the time goes in v1:
time: 153 us; the launch traced here: 152 us
  Pallas kernels  146 us (95%)
  local copies, waits for them, and re-layouts  6.2 us (4%)
    pallas_call x1, Pallas kernels, local(): pl.pallas_call(kernel, out_shape=[jax.ShapeDtypeStruct((32, rows), F32)]...  146 us
    unnamed x4, local copies, waits for them, and re-layouts  6.2 us

profile of v1, /device:TPU:1, one launch (start us, length us, event | category | flops | bytes accessed | tf_op | source)
XLA Modules:
  0.0 152.5 jit_solution(16616714218403256214)
XLA Ops:
  0.6 145.6 %shard_map.102 = (f32[32,864]{1,0:T(8,128)}, f32[32,864]{1,0:T(8,128)}, f32[32,864]{1,0:T(8,128)}, f32[32,864]{1,0:T(8,128)}) custom-call(f32[864,1728]{1,0:T(8,128)} %bitcast.21, f32[864,1728]{1,0:T(8,128)} %bitcast.22, f32[32,864]{1,0:T(8,128)} %bitcast.23, f32[32,864]{1,0:T(8,128)} %bitcast.24, s32[32,864]{1,0:T(8,128)} %bitcast.25, ...), custom_call_target="tpu_custom_call" | custom-call | tf_op jit(solution)/shard_map/pallas_call | solution.py:338
  146.3 1.6 %copy.15 = f32[1,864,32]{1,2,0:T(8,128)} copy(f32[1,864,32]{1,2,0:T(8,128)} %bitcast.29) | data formatting | bytes 221184
  147.8 1.6 %copy.16 = f32[1,864,32]{1,2,0:T(8,128)} copy(f32[1,864,32]{1,2,0:T(8,128)} %bitcast.28) | data formatting | bytes 221184
  149.4 1.6 %copy.17 = f32[1,864,32]{1,2,0:T(8,128)} copy(f32[1,864,32]{1,2,0:T(8,128)} %bitcast.27) | data formatting | bytes 221184
  150.9 1.6 %copy.18 = f32[1,864,32]{1,2,0:T(8,128)} copy(f32[1,864,32]{1,2,0:T(8,128)} %bitcast.26) | data formatting | bytes 221184

commit v2 on v1

--- a/solution.py
+++ b/solution.py
@@ -62,11 +62,11 @@
 
 
 def kernel(
-    rre, rim, fre, fim, fa, t1, t2,
+    rre, rim, fre_h, fim_h, fa_h, t1_h, t2_h,
     mre, mim, pre, pim,
-    stage, rcat, acc, fsend, relay1, gbuf, bsend, relay2, urecv, fasend, farecv,
-    ld_sem, ini_send, ini_recv, fa_send, fa_recv,
-    f1_send, f1_recv, f2_send, f2_recv, b1_send, b1_recv, b2_send, b2_send2, b2_recv,
+    stage, fbuf, fa, t1, t2, rcat, acc, fsend, gbuf, bsend, relay2, urecv, fasend, farecv,
+    ld_sem, in_sem, ini_send, ini_recv, fa_send, fa_recv,
+    f_send, f_recv, b1_send, b1_recv, b2_send, b2_send2, b2_recv,
 ):
     me = lax.axis_index("freq")
     row = lax.axis_index("row")
@@ -83,16 +83,14 @@
     def dev(xi, zi, yi, ci):
         return (xi * 32 + zi * 4 + (yi // 2) * 2 + ci, lax.rem(yi, 2))
 
-    plane = [(dx, dy, dc) for dx in (2, 1, 3, 0) for dy in (2, 1, 3, 0) for dc in (1, 0)][:-1]
-    zorder = [4, 3, 5, 2, 6, 1, 7]
-    barrier = pltpu.get_barrier_semaphore()
-    for dx, dy, dc in plane:
-        pl.semaphore_signal(
-            barrier, inc=1, device_id=dev(xs[dx], z, ys[dy], cs[dc]), device_id_type=MESH
+    loads = [
+        pltpu.make_async_copy(src, dst, in_sem.at[i])
+        for i, (src, dst) in enumerate(
+            ((fre_h, fbuf.at[0]), (fim_h, fbuf.at[1]), (fa_h, fa), (t1_h, t1), (t2_h, t2))
         )
-    for dz in zorder:
-        pl.semaphore_signal(barrier, inc=1, device_id=dev(x, zs[dz], ypos, c), device_id_type=MESH)
-
+    ]
+    for load in loads:
+        load.start()
     nchunk = rre.shape[0] // CHUNK
     for k in range(nchunk):
         for a, ref in enumerate((rre, rim)):
@@ -102,14 +100,28 @@
                 ld_sem.at[k, a],
             ).start()
 
+    xorder, zorder = (2, 1, 3, 0), (4, 3, 5, 2, 6, 1, 7)
+    away = [
+        (dx, dy, dz, dc) for dz in (*zorder, 0) for dx in xorder for dy in (1, 3) for dc in (1, 0)
+    ]
+    away += [(dx, dy, 0, dc) for dx in xorder for dy in (2, 0) for dc in (1, 0)][:-1]
+    away += [(0, 0, dz, 0) for dz in zorder]
+    barrier = pltpu.get_barrier_semaphore()
+    for dx, dy, dz, dc in away:
+        pl.semaphore_signal(
+            barrier, inc=1, device_id=dev(xs[dx], zs[dz], ys[dy], cs[dc]), device_id_type=MESH
+        )
+
     u2 = urecv.reshape(5 * 8 * 128, 128)
+    for load in loads[:3]:
+        load.wait()
     for q in range(4):
         base = (row * 4 + q) * 128
         for h in range(2):
             n = 128 if h == 0 else BLK - 128
             lo = BLK * q + 128 * h
-            for ri, ref in enumerate((fre, fim)):
-                v = ref[:, lo : lo + n]
+            for ri in range(2):
+                v = fbuf[ri, :, lo : lo + n]
                 if n < 128:
                     v = jnp.concatenate([v, jnp.zeros((32, 128 - n), F32)], axis=1)
                 u2[pl.ds(base + 2 * h + ri, 32, stride=4), :] = v
@@ -124,7 +136,7 @@
     for h in range(2):
         fasend[8 * h : 8 * h + 8] = jnp.broadcast_to(w[:, 128 * h : 128 * h + 128], (8, 128))
 
-    pl.semaphore_wait(barrier, len(plane) + len(zorder))
+    pl.semaphore_wait(barrier, len(away))
     partner = (me, 1 - row)
     mine = urecv.at[0, pl.ds(row * 4, 4)]
     ini = copies(mine, mine, ini_send, ini_recv, partner)
@@ -147,6 +159,8 @@
     lax.fori_loop(0, nchunk, convert, 0)
     acc[864:, :] = jnp.zeros_like(acc[864:, :])
     fac.wait()
+    for load in loads[3:]:
+        load.wait()
 
     f1v = fsend.reshape(ITERS * 512, 128)
     g2 = gbuf.reshape(ITERS * 512, 128)
@@ -225,27 +239,16 @@
                         f1v[pl.ds(it * 512 + q * 128 + 2 * h + ri, 32, stride=4), :] = v[
                             32 * ri : 32 * ri + 32
                         ]
-                for dx in (2, 1, 3, 0):
-                    copies(
-                        fsend.at[it, q, xs[dx]],
-                        relay1.at[it, yh, sid],
-                        f1_send.at[it],
-                        f1_recv.at[it, yh],
-                        dev(xs[dx], z, yi, cd),
-                    ).start()
-        for dy in (3, 1):
-            v = ys[dy] // 2
-            wait_bytes(relay1.at[it, v], f1_recv.at[it, v])
-            for dz in zorder:
-                copies(
-                    relay1.at[it, v, :, zs[dz]],
-                    gbuf.at[it, z, v],
-                    f2_send.at[it],
-                    f2_recv.at[it],
-                    dev(x, zs[dz], ypos, c),
-                ).start()
-            gbuf[it, z, v] = relay1[it, v, :, z]
-        wait_bytes(gbuf.at[it, pl.ds(0, 7)], f2_recv.at[it])
+                for dz in (*zorder, 0):
+                    for dx in xorder:
+                        copies(
+                            fsend.at[it, q, xs[dx], zs[dz]],
+                            gbuf.at[it, z, yh, sid],
+                            f_send.at[it],
+                            f_recv.at[it],
+                            dev(xs[dx], zs[dz], yi, cd),
+                        ).start()
+        wait_bytes(gbuf.at[it], f_recv.at[it])
 
         g = jnp.concatenate(
             [
@@ -288,36 +291,28 @@
 
         for near, v in enumerate((1 - yh, yh)):
             wait_bytes(relay2.at[it, v, pl.ds(0, 7)], b1_recv.at[it, v])
-            for dx in (2, 1, 3, 0):
+            for dx in xorder:
                 for dc in (1, 0):
                     out_to(dx, v, 1 - row, dc, b2_send.at[it])
 
             @pl.when(it < ITERS - 1)
             def _():
-                for dx in (2, 1, 3, 0):
+                for dx in xorder:
                     for dc in (1, 0):
                         if near and dx == 0 and dc == 0:
                             urecv[it + 1, myn, x] = relay2[it, v, :, sid]
                         else:
                             out_to(dx, v, row, dc, b2_send2.at[it])
 
-        wait_bytes(fsend.at[it], f1_send.at[it])
-        wait_bytes(gbuf.at[it, pl.ds(0, 7)], f2_send.at[it])
-        wait_bytes(gbuf.at[it, pl.ds(0, 7)], b1_send.at[it])
-        wait_bytes(ublk.at[pl.ds(0, 16)], b2_send.at[it])
-
-        @pl.when(it < ITERS - 1)
-        def _():
-            wait_bytes(ublk.at[pl.ds(0, 15)], b2_send2.at[it])
-
         return carry
 
     lax.fori_loop(0, ITERS, apply, 0)
 
-    for q in range(4):
-        n = row * 4 + q
-        wait_bytes(urecv.at[ITERS, n], b2_recv.at[ITERS, n])
-        for slot, outs in ((ITERS - 1, (mre, mim)), (ITERS, (pre, pim))):
+    def result(slot, outs):
+        for q in range(4):
+            n = row * 4 + q
+            if slot == ITERS:
+                wait_bytes(urecv.at[ITERS, n], b2_recv.at[ITERS, n])
             for h in range(2):
                 m = 128 if h == 0 else BLK - 128
                 lo = BLK * q + 128 * h
@@ -328,6 +323,20 @@
                         v = v + u2[pl.ds(n * 128 + j, 32, stride=4), :]
                     outs[ri][:, lo : lo + m] = v[:, 0:m]
 
+    result(ITERS - 1, (mre, mim))
+    for it in range(ITERS):
+        wait_bytes(fsend.at[it], f_send.at[it])
+        wait_bytes(gbuf.at[it, pl.ds(0, 7)], b1_send.at[it])
+        wait_bytes(ublk.at[pl.ds(0, 16)], b2_send.at[it])
+        if it < ITERS - 1:
+            wait_bytes(ublk.at[pl.ds(0, 15)], b2_send2.at[it])
+    result(ITERS, (pre, pim))
+
+
+def hand_on(*refs):
+    for i in range(4):
+        refs[4 + i][...] = refs[i][...]
+
 
 def local(reflect_re, reflect_im, focus_re, focus_im, first_arrival):
     rows, cols = reflect_re.shape[1:]
@@ -338,23 +347,26 @@
     outs = pl.pallas_call(
         kernel,
         out_shape=[jax.ShapeDtypeStruct((32, rows), F32)] * 4,
-        in_specs=[hbm, hbm] + [vmem] * 5,
+        in_specs=[hbm] * 7,
         out_specs=[vmem] * 4,
         scratch_shapes=[
             pltpu.VMEM((2, rows, cols), F32),
+            pltpu.VMEM((2, 32, rows), F32),
+            pltpu.VMEM((32, rows), jnp.int32),
+            pltpu.VMEM(t1.shape, BF16),
+            pltpu.VMEM(t2.shape, BF16),
             pltpu.VMEM((8, rows, 1024), BF16),
             pltpu.VMEM((rows + 48, 128), F32),
             pltpu.VMEM((ITERS, 4, 4, 8, 4, 128), F32),
-            pltpu.VMEM((ITERS, 2, 8, 8, 4, 128), F32),
             pltpu.VMEM((ITERS, 8, 2, 8, 4, 128), F32),
             pltpu.VMEM((ITERS, 8, 2, 8, 4, 128), F32),
             pltpu.VMEM((ITERS, 2, 8, 8, 4, 128), F32),
             pltpu.VMEM((5, 8, 4, 8, 4, 128), F32),
             pltpu.VMEM((16, 128), F32),
             pltpu.VMEM((16, 128), F32),
-            dma((rows // CHUNK, 2)),
+            dma((rows // CHUNK, 2)), dma((5,)),
             dma, dma, dma, dma,
-            dma((ITERS,)), dma((ITERS, 2)), dma((ITERS,)), dma((ITERS,)),
+            dma((ITERS,)), dma((ITERS,)),
             dma((ITERS,)), dma((ITERS, 2)), dma((ITERS,)), dma((ITERS,)),
             dma((5, 8)),
         ],
@@ -365,6 +377,12 @@
         reflect_re[0], reflect_im[0], focus_re[0].T, focus_im[0].T, first_arrival.T,
         jnp.asarray(t1), jnp.asarray(t2),
     )
+    outs = pl.pallas_call(
+        hand_on,
+        out_shape=[jax.ShapeDtypeStruct((32, rows), F32)] * 4,
+        in_specs=[vmem] * 4,
+        out_specs=[vmem] * 4,
+    )(*outs)
     return tuple(o.T[None] for o in outs)
 
 

time: 153 us -> 140 us (0.915)
  Pallas kernels: 146 us -> 139 us
  local copies, waits for them, and re-layouts: 6.2 us -> 0 us
    pallas_call x1, Pallas kernels: 146 us -> 137 us  [local(): pl.pallas_call(kernel, out_shape=[jax.ShapeDtypeStruct((32, rows), F32)]...]
    unnamed x4 -> x0, local copies, waits for them, and re-layouts: 6.2 us -> none
    pallas_call x0 -> x1, Pallas kernels: none -> 1.84 us  [local(): pl.pallas_call(hand_on, out_shape=[jax.ShapeDtypeStruct((32, rows), F32)]...]
where the time goes in v2:
time: 140 us
  Pallas kernels  139 us (99%)
    pallas_call x1, Pallas kernels, local(): pl.pallas_call(kernel, out_shape=[jax.ShapeDtypeStruct((32, rows), F32)]...  137 us

profile of v2, /device:TPU:1, one launch (start us, length us, event | category | flops | bytes accessed | tf_op | source)
XLA Modules:
  0.0 139.9 jit_solution(12338347681830774996)
XLA Ops:
  0.6 137.5 %shard_map.102 = (f32[32,864]{1,0:T(8,128)}, f32[32,864]{1,0:T(8,128)}, f32[32,864]{1,0:T(8,128)}, f32[32,864]{1,0:T(8,128)}) custom-call(f32[864,1728]{1,0:T(8,128)} %bitcast.21, f32[864,1728]{1,0:T(8,128)} %bitcast.22, f32[32,864]{1,0:T(8,128)} %bitcast.23, f32[32,864]{1,0:T(8,128)} %bitcast.24, s32[32,864]{1,0:T(8,128)} %bitcast.25, ...), custom_call_target="tpu_custom_call" | custom-call | tf_op jit(solution)/shard_map/pallas_call | solution.py:347
  138.1 1.8 %shard_map.103 = (f32[32,864]{1,0:T(8,128)}, f32[32,864]{1,0:T(8,128)}, f32[32,864]{1,0:T(8,128)}, f32[32,864]{1,0:T(8,128)}) custom-call(f32[32,864]{1,0:T(8,128)} %get-tuple-element.12.refs_0_, f32[32,864]{1,0:T(8,128)} %get-tuple-element.13.refs_1_, f32[32,864]{1,0:T(8,128)} %get-tuple-element.14.refs_2_, f32[32,864]{1,0:T(8,128)} %get-tuple-element.15.refs_3_), custom_call_target="tpu_custom_call" | custom-call | tf_op jit(solution)/shard_map/pallas_call | solution.py:380

commit v3 on v2

--- a/solution.py
+++ b/solution.py
@@ -29,8 +29,8 @@
             x * 32 + z * 4 + y * 2 + c
             for z in range(8)
             for y in range(2)
+            for c in range(2)
             for x in range(4)
-            for c in range(2)
         ]
     )
     t = np.arange(256)
@@ -79,6 +79,8 @@
     zs = [lax.rem(z + d, 8) for d in range(8)]
     ys = [lax.rem(ypos + d, 4) for d in range(4)]
     cs = [c, 1 - c]
+
+    xf, zf = [v * 32 for v in xs], [v * 4 for v in zs]
 
     def dev(xi, zi, yi, ci):
         return (xi * 32 + zi * 4 + (yi // 2) * 2 + ci, lax.rem(yi, 2))
@@ -166,7 +168,6 @@
     g2 = gbuf.reshape(ITERS * 512, 128)
     bs2 = bsend.reshape(ITERS * 512, 128)
     ublk = urecv.reshape(5 * 32, 8, 4, 128)
-    sid = x * 2 + c
     myn = (1 - row) * 4 + myq
     reach = jnp.concatenate([farecv[0:1], farecv[8:9]], axis=1)
     tid = lax.broadcasted_iota(jnp.int32, (256, 256), 0)
@@ -178,9 +179,9 @@
 
         def block(t, first):
             v = t // 2
-            ci = lax.rem(c + t + 1, 2)
+            ci = lax.rem(c + 1 + jnp.where(it == 0, t, v), 2)
             y_own = 2 * (v % 2) + lax.rem(row + 1 + v // 2, 2)
-            y_arr = 2 * lax.rem(yh + 1 + v // 2, 2) + lax.rem(row + 1 + v % 2, 2)
+            y_arr = 2 * lax.rem(yh + 1 + v // 2, 2) + lax.rem(row + 1 + t, 2)
             yi = jnp.where(it == 0, y_own, y_arr)
             n = (1 - lax.rem(yi, 2)) * 4 + (yi // 2) * 2 + ci
 
@@ -231,7 +232,8 @@
         for dy in (1, 3):
             yi = ys[dy]
             for cd in range(2):
-                q = (yi // 2) * 2 + cd
+                base, par = (yi // 2) * 2 + cd, lax.rem(yi, 2)
+                q = base
                 for h in range(2):
                     v = acc[pl.ds(pl.multiple_of(BLK * q + 128 * h, 8), 128), :].T
                     v = v[0:64] + v[64:128]
@@ -243,10 +245,10 @@
                     for dx in xorder:
                         copies(
                             fsend.at[it, q, xs[dx], zs[dz]],
-                            gbuf.at[it, z, yh, sid],
+                            gbuf.at[it, z, yh, c, x],
                             f_send.at[it],
                             f_recv.at[it],
-                            dev(xs[dx], zs[dz], yi, cd),
+                            (xf[dx] + (zf[dz] + base), par),
                         ).start()
         wait_bytes(gbuf.at[it], f_recv.at[it])
 
@@ -269,40 +271,39 @@
                 bs2[pl.ds(it * 512 + 2 * h + ri, 128, stride=4), :] = out[
                     128 * ri : 128 * ri + 128, 128 * h : 128 * h + 128
                 ]
-        for v in (1 - yh, yh):
+        parts = ((1 - yh, 1 - c), (1 - yh, c), (yh, 1 - c), (yh, c))
+        for i, (v, cc) in enumerate(parts):
             for dz in zorder:
                 copies(
-                    bsend.at[it, zs[dz], v],
-                    relay2.at[it, v, z],
+                    bsend.at[it, zs[dz], v, cc],
+                    relay2.at[it, v, cc, z],
                     b1_send.at[it],
-                    b1_recv.at[it, v],
+                    b1_recv.at[it, i],
                     dev(x, zs[dz], ypos, c),
                 ).start()
-            relay2[it, v, z] = bsend[it, z, v]
-
-        def out_to(dx, v, r, dc, sem):
+            relay2[it, v, cc, z] = bsend[it, z, v, cc]
+
+        def out_to(dx, v, cc, r, sem):
             copies(
-                relay2.at[it, v, :, xs[dx] * 2 + cs[dc]],
+                relay2.at[it, v, cc, :, xs[dx]],
                 urecv.at[it + 1, myn, x],
                 sem,
                 b2_recv.at[it + 1, myn],
-                dev(xs[dx], z, 2 * v + r, cs[dc]),
+                dev(xs[dx], z, 2 * v + r, cc),
             ).start()
 
-        for near, v in enumerate((1 - yh, yh)):
-            wait_bytes(relay2.at[it, v, pl.ds(0, 7)], b1_recv.at[it, v])
+        for i, (v, cc) in enumerate(parts):
+            wait_bytes(relay2.at[it, v, cc, pl.ds(0, 7)], b1_recv.at[it, i])
             for dx in xorder:
-                for dc in (1, 0):
-                    out_to(dx, v, 1 - row, dc, b2_send.at[it])
+                out_to(dx, v, cc, 1 - row, b2_send.at[it])
 
             @pl.when(it < ITERS - 1)
             def _():
                 for dx in xorder:
-                    for dc in (1, 0):
-                        if near and dx == 0 and dc == 0:
-                            urecv[it + 1, myn, x] = relay2[it, v, :, sid]
-                        else:
-                            out_to(dx, v, row, dc, b2_send2.at[it])
+                    if i == 3 and dx == 0:
+                        urecv[it + 1, myn, x] = relay2[it, v, cc, :, x]
+                    else:
+                        out_to(dx, v, cc, row, b2_send2.at[it])
 
         return carry
 
@@ -358,16 +359,16 @@
             pltpu.VMEM((8, rows, 1024), BF16),
             pltpu.VMEM((rows + 48, 128), F32),
             pltpu.VMEM((ITERS, 4, 4, 8, 4, 128), F32),
-            pltpu.VMEM((ITERS, 8, 2, 8, 4, 128), F32),
-            pltpu.VMEM((ITERS, 8, 2, 8, 4, 128), F32),
-            pltpu.VMEM((ITERS, 2, 8, 8, 4, 128), F32),
+            pltpu.VMEM((ITERS, 8, 2, 2, 4, 4, 128), F32),
+            pltpu.VMEM((ITERS, 8, 2, 2, 4, 4, 128), F32),
+            pltpu.VMEM((ITERS, 2, 2, 8, 4, 4, 128), F32),
             pltpu.VMEM((5, 8, 4, 8, 4, 128), F32),
             pltpu.VMEM((16, 128), F32),
             pltpu.VMEM((16, 128), F32),
             dma((rows // CHUNK, 2)), dma((5,)),
             dma, dma, dma, dma,
             dma((ITERS,)), dma((ITERS,)),
-            dma((ITERS,)), dma((ITERS, 2)), dma((ITERS,)), dma((ITERS,)),
+            dma((ITERS,)), dma((ITERS, 4)), dma((ITERS,)), dma((ITERS,)),
             dma((5, 8)),
         ],
         compiler_params=pltpu.CompilerParams(

time: 140 us -> 136 us (0.971)
  Pallas kernels: 139 us -> 135 us
    pallas_call x1, Pallas kernels: 137 us -> 133 us  [local(): pl.pallas_call(kernel, out_shape=[jax.ShapeDtypeStruct((32, rows), F32)]...]
where the time goes in v3:
time: 136 us
  Pallas kernels  135 us (99%)
    pallas_call x1, Pallas kernels, local(): pl.pallas_call(kernel, out_shape=[jax.ShapeDtypeStruct((32, rows), F32)]...  133 us

profile of v3, /device:TPU:1, one launch (start us, length us, event | category | flops | bytes accessed | tf_op | source)
XLA Modules:
  0.0 135.9 jit_solution(9073646895668809064)
XLA Ops:
  0.6 133.5 %shard_map.102 = (f32[32,864]{1,0:T(8,128)}, f32[32,864]{1,0:T(8,128)}, f32[32,864]{1,0:T(8,128)}, f32[32,864]{1,0:T(8,128)}) custom-call(f32[864,1728]{1,0:T(8,128)} %bitcast.21, f32[864,1728]{1,0:T(8,128)} %bitcast.22, f32[32,864]{1,0:T(8,128)} %bitcast.23, f32[32,864]{1,0:T(8,128)} %bitcast.24, s32[32,864]{1,0:T(8,128)} %bitcast.25, ...), custom_call_target="tpu_custom_call" | custom-call | tf_op jit(solution)/shard_map/pallas_call | solution.py:348
  134.1 1.8 %shard_map.103 = (f32[32,864]{1,0:T(8,128)}, f32[32,864]{1,0:T(8,128)}, f32[32,864]{1,0:T(8,128)}, f32[32,864]{1,0:T(8,128)}) custom-call(f32[32,864]{1,0:T(8,128)} %get-tuple-element.12.refs_0_, f32[32,864]{1,0:T(8,128)} %get-tuple-element.13.refs_1_, f32[32,864]{1,0:T(8,128)} %get-tuple-element.14.refs_2_, f32[32,864]{1,0:T(8,128)} %get-tuple-element.15.refs_3_), custom_call_target="tpu_custom_call" | custom-call | tf_op jit(solution)/shard_map/pallas_call | solution.py:381

commit v4 on v3

--- a/solution.py
+++ b/solution.py
@@ -140,9 +140,9 @@
 
     pl.semaphore_wait(barrier, len(away))
     partner = (me, 1 - row)
-    mine = urecv.at[0, pl.ds(row * 4, 4)]
-    ini = copies(mine, mine, ini_send, ini_recv, partner)
-    ini.start()
+    for q in (1 - c, c, 3 - c, 2 + c):
+        mine = urecv.at[0, row * 4 + q]
+        copies(mine, mine, ini_send, ini_recv.at[q], partner).start()
     fac = copies(fasend, farecv, fa_send, fa_recv, partner)
     fac.start()
 
@@ -193,9 +193,9 @@
             def _():
                 wait_bytes(urecv.at[it, n, pl.ds(0, 3)], b2_recv.at[it, n])
 
-            @pl.when((it == 0) & (t == 4))
+            @pl.when((it == 0) & (t >= 4))
             def _():
-                ini.wait()
+                wait_bytes(urecv.at[0, n], ini_recv.at[(yi // 2) * 2 + ci])
 
             parts = []
             for ri in range(2):
@@ -325,6 +325,7 @@
                     outs[ri][:, lo : lo + m] = v[:, 0:m]
 
     result(ITERS - 1, (mre, mim))
+    wait_bytes(urecv.at[0, pl.ds(0, 4)], ini_send)
     for it in range(ITERS):
         wait_bytes(fsend.at[it], f_send.at[it])
         wait_bytes(gbuf.at[it, pl.ds(0, 7)], b1_send.at[it])
@@ -366,7 +367,7 @@
             pltpu.VMEM((16, 128), F32),
             pltpu.VMEM((16, 128), F32),
             dma((rows // CHUNK, 2)), dma((5,)),
-            dma, dma, dma, dma,
+            dma, dma((4,)), dma, dma,
             dma((ITERS,)), dma((ITERS,)),
             dma((ITERS,)), dma((ITERS, 4)), dma((ITERS,)), dma((ITERS,)),
             dma((5, 8)),

time: 136 us -> 136 us (level)
  no operation moved by 1% of the time
where the time goes in v4:
time: 136 us
  Pallas kernels  135 us (99%)
    pallas_call x1, Pallas kernels, local(): pl.pallas_call(kernel, out_shape=[jax.ShapeDtypeStruct((32, rows), F32)]...  133 us

profile of v4, /device:TPU:1, one launch (start us, length us, event | category | flops | bytes accessed | tf_op | source)
XLA Modules:
  0.0 135.9 jit_solution(14133580129137967626)
XLA Ops:
  0.6 133.4 %shard_map.102 = (f32[32,864]{1,0:T(8,128)}, f32[32,864]{1,0:T(8,128)}, f32[32,864]{1,0:T(8,128)}, f32[32,864]{1,0:T(8,128)}) custom-call(f32[864,1728]{1,0:T(8,128)} %bitcast.21, f32[864,1728]{1,0:T(8,128)} %bitcast.22, f32[32,864]{1,0:T(8,128)} %bitcast.23, f32[32,864]{1,0:T(8,128)} %bitcast.24, s32[32,864]{1,0:T(8,128)} %bitcast.25, ...), custom_call_target="tpu_custom_call" | custom-call | tf_op jit(solution)/shard_map/pallas_call | solution.py:349
  134.0 1.8 %shard_map.103 = (f32[32,864]{1,0:T(8,128)}, f32[32,864]{1,0:T(8,128)}, f32[32,864]{1,0:T(8,128)}, f32[32,864]{1,0:T(8,128)}) custom-call(f32[32,864]{1,0:T(8,128)} %get-tuple-element.12.refs_0_, f32[32,864]{1,0:T(8,128)} %get-tuple-element.13.refs_1_, f32[32,864]{1,0:T(8,128)} %get-tuple-element.14.refs_2_, f32[32,864]{1,0:T(8,128)} %get-tuple-element.15.refs_3_), custom_call_target="tpu_custom_call" | custom-call | tf_op jit(solution)/shard_map/pallas_call | solution.py:382
